TPU v7x, 32 devices: a whole 2x2x4 slice. The times are simulated.
32 devices in a mesh: freq: 8 (over z, x), kgrp: 4 (over y, core).
Axes of the slice: x: 2, y: 2, z: 4, core: 2. Of those that a mesh axis runs over, the one named last changes fastest.
Arguments:
- hamiltonian: float32 [256, 64, 128], P(('freq', 'kgrp')), may hold values from -1 to 1, as said below
- self_energy: float32 [16, 64, 128], P('freq'), may hold values from -0.8 to 0.3, as said below
- guess_factor: float32 [16, 64, 128], P('freq'), may hold values from -0.05 to 1.25
- weights: int32 [256], replicated, may hold values from 1 to 48
- counts: int32 [16], replicated, may hold values from 1 to 3, as said below
Outputs:
- local_green: float32 [4096, 32], P(('freq', 'kgrp'))
Inputs may be any that keep to these rules, and one draw needn't show every extreme that they name: `hamiltonian`: each k-point's matrix is Hermitian: the left half symmetric, the right half antisymmetric. `self_energy`: the diagonal of the right half lies between -0.8 and -0.4. `counts`: the number of Newton-Schulz steps taken at each frequency.
All inputs are finite; a program needn't handle non-finite values.
Results may differ from a plain program's by a relative error of at most 0.0001.
Values sent between devices are 32-bit elements.
No kernel may reach another device: no remote copies, remote signals or barrier semaphores. Data moves between devices by JAX's collectives and lax.ppermute only.
A program may use at most 64 MiB of HBM per device.

v0:
```python
import functools
import math

import jax
import jax.numpy as jnp
from jax import lax
from jax.experimental import pallas as pl
from jax.experimental.pallas import tpu as pltpu
from jax.sharding import PartitionSpec as P


chem_potential = 0.2
BATCH = 8
COST = 400_000_000


def is_power_of_two(number):
    return number & (number - 1) == 0


def split_bf16(values):
    high = values.astype(jnp.bfloat16)
    low = (values - high.astype(jnp.float32)).astype(jnp.bfloat16)
    return high, low


def swap_halves(values):
    return pltpu.roll(values, values.shape[-1] // 2, 1)


def block_form(values, swap_sign):
    return jnp.concatenate([values, swap_halves(values) * swap_sign], 0)


def split_block(values, swap_sign):
    high, low = split_bf16(values)
    sign = swap_sign.astype(jnp.bfloat16)
    return (
        jnp.concatenate([high, swap_halves(high) * sign], 0),
        jnp.concatenate([low, swap_halves(low) * sign], 0),
    )


def left_tile(high, low):
    return jnp.concatenate([high, low], -1)


def right_tile(high, low):
    upper = jnp.concatenate([high, low], -1)
    lower = jnp.concatenate([high, jnp.zeros_like(low)], -1)
    return jnp.concatenate([upper, lower], 0)


def add_halves(both):
    width = both.shape[-1] // 2
    return both[:, :width] + both[:, width:]


def product(left, right):
    return add_halves(jnp.dot(left, right, preferred_element_type=jnp.float32))


class Layout:
    def __init__(self, hamiltonian, self_energy):
        self.k_local, self.orbitals, self.width = hamiltonian.shape
        per_freq = self_energy.shape[0]
        self.freq_devs = lax.axis_size("freq")
        self.group_devs = lax.axis_size("kgrp")
        self.freq_total = per_freq * self.freq_devs
        self.x_devs = 2 if self.freq_devs % 2 == 0 else 1
        self.c_devs = 2 if self.group_devs % 2 == 0 and per_freq % 2 == 0 else 1
        self.z_devs = self.freq_devs // self.x_devs
        self.y_devs = self.group_devs // self.c_devs
        self.sub = per_freq // self.c_devs
        self.freqs = self.z_devs * self.sub
        self.lead_steps = min(2, self.z_devs)
        self.lead = self.lead_steps * self.sub

    def positions(self):
        freq_pos = lax.axis_index("freq")
        group_pos = lax.axis_index("kgrp")
        return freq_pos, group_pos, group_pos % self.c_devs

    def block_of(self, step):
        z_pos = lax.axis_index("freq") // self.x_devs
        if is_power_of_two(self.z_devs):
            return z_pos ^ step
        return (z_pos + self.z_devs - step) % self.z_devs

    def freq_of(self, place):
        freq_pos, _, c_pos = self.positions()
        block = self.block_of(place // self.sub) * self.x_devs + freq_pos % self.x_devs
        return block * (self.c_devs * self.sub) + c_pos * self.sub + place % self.sub

    def matsubara(self, place):
        return (2 * self.freq_of(place) + 1).astype(jnp.float32) * (math.pi / (2 * self.freq_total))

    def plane_of(self, place):
        return self.block_of(place // self.sub) * self.sub + place % self.sub


class Masks:
    def __init__(self, orbitals):
        width = 2 * orbitals
        row = lax.broadcasted_iota(jnp.int32, (orbitals, width), 0)
        lane = lax.broadcasted_iota(jnp.int32, (orbitals, width), 1)
        self.eye_left = (lane == row).astype(jnp.float32)
        self.eye_right = (lane == row + orbitals).astype(jnp.float32)
        self.eye_both = self.eye_left + self.eye_right
        self.eye_block = jnp.concatenate([self.eye_left, self.eye_right], 0)
        self.left_row = lax.broadcasted_iota(jnp.int32, (1, width), 1) < orbitals
        self.sign = jnp.where(self.left_row, -1.0, 1.0)


def prepare_frequency(plan, masks, place, sigma, guess, target, left_ref, right_ref, shift_ref, rows_ref):
    orbitals = plan.orbitals
    matsubara = plan.matsubara(place)
    high, low = split_bf16(block_form(guess, masks.sign))
    left = left_tile(high[:orbitals], low[:orbitals])
    left_ref[pl.ds(target * orbitals, orbitals), :] = left
    right_ref[target] = left_tile(high, low)
    energy = masks.eye_left * chem_potential + masks.eye_right * matsubara
    matrix = split_bf16(block_form(energy - sigma, masks.sign))
    shift_ref[target] = product(left, right_tile(*matrix))
    sigma_diag = jnp.sum(sigma * masks.eye_both, 0, keepdims=True)
    sigma_swap = swap_halves(sigma_diag)
    real = chem_potential - jnp.where(masks.left_row, sigma_diag, sigma_swap)
    imag = matsubara - jnp.where(masks.left_row, sigma_swap, sigma_diag)
    rows_ref[target, pl.ds(0, 1), :] = real
    rows_ref[target, pl.ds(1, 1), :] = imag


def diagonal_row(masks, matrix):
    diag = jnp.sum(matrix * masks.eye_left, 0, keepdims=True)
    return diag + swap_halves(diag)


def sum_points(plan, masks, rows, constant, load_t, diags, weights, total):
    orbitals = plan.orbitals
    real = rows[0:1] - diags
    imag = jnp.broadcast_to(rows[1:2], real.shape)
    modulus = real * real + imag * imag
    d_real = real / modulus
    d_imag = -imag / modulus
    d_start = jnp.where(masks.left_row, d_real, d_imag) * weights
    d_turned = d_imag * masks.sign
    d_signed = d_real * masks.sign

    def errors_of(items):
        errors = []
        for item in items:
            mixed = constant - load_t(item)
            turned = swap_halves(mixed)
            upper = mixed * d_real[item:item + 1] + turned * d_turned[item:item + 1]
            lower = turned * d_signed[item:item + 1] - mixed * d_imag[item:item + 1]
            errors.append(split_bf16(masks.eye_block - jnp.concatenate([upper, lower], 0)))
        return errors

    def advance(series, powers):
        next_series, next_powers = [], []
        for start, (high, low) in zip(series, powers):
            s_high, s_low = split_bf16(start)
            stacked = jnp.concatenate([left_tile(s_high, s_low), left_tile(high[:orbitals], low[:orbitals])], 0)
            both = product(stacked, right_tile(high, low))
            next_series.append(start + both[:orbitals])
            next_powers.append(split_block(both[orbitals:], masks.sign))
        return next_series, next_powers

    def finish(total, series, powers):
        lefts = [left_tile(*split_bf16(start)) for start in series]
        rights = [right_tile(*power) for power in powers]
        for start in series:
            total = total + start
        return total + product(jnp.concatenate(lefts, 1), jnp.concatenate(rights, 0))

    def accumulate(advances, total):
        for begin in range(0, plan.k_total, BATCH):
            items = range(begin, min(begin + BATCH, plan.k_total))
            series = [masks.eye_both * d_start[item:item + 1] for item in items]
            powers = errors_of(items)
            for _ in range(advances):
                series, powers = advance(series, powers)
            total = finish(total, series, powers)
        return total

    return lambda advances: accumulate(advances, total)


def run_counts(count, accumulate, store):
    @pl.when(count <= 1)
    def _():
        store(accumulate(0))

    @pl.when(count == 2)
    def _():
        store(accumulate(1))

    @pl.when(count >= 3)
    def _():
        store(accumulate(2))


def fetch(source_ref, target_ref, semaphore):
    copy = pltpu.make_async_copy(source_ref, target_ref, semaphore)
    copy.start()
    return copy


def first_kernel(plan, flips, weights_ref, counts_ref, own_ref, *refs):
    k_local, orbitals = plan.k_local, plan.orbitals
    sg_refs, refs = refs[:plan.lead_steps], refs[plan.lead_steps:]
    mates = len(flips[0]) - 1
    mate_refs, refs = refs[:mates], refs[mates:]
    sum_ref, left_ref, right_ref, shift_ref, rows_ref, hs_ref, hd_ref, wr_ref = refs[:8]
    t_ref, h_ref, weight_ref, count_ref, sems = refs[8:]
    masks = Masks(orbitals)
    own_copy = fetch(own_ref, h_ref, sems.at[0])
    weight_copy = fetch(weights_ref, weight_ref, sems.at[1])
    count_copy = fetch(counts_ref, count_ref, sems.at[2])
    freq_pos, group_pos, _ = plan.positions()
    for place in range(plan.lead):
        sg_ref = sg_refs[place // plan.sub]
        member = place % plan.sub
        prepare_frequency(
            plan, masks, place, sg_ref[0, member], sg_ref[1, member], place,
            left_ref, right_ref, shift_ref, rows_ref,
        )

    def load_piece(piece, source_ref):
        for local in range(k_local):
            place = piece * k_local + local
            matrix = source_ref[local]
            high, low = split_bf16(block_form(matrix, masks.sign))
            hs_ref[place] = left_tile(high, low)
            hd_ref[pl.ds(place, 1), :] = diagonal_row(masks, matrix)
            t_ref[place] = product(left_ref[...], right_tile(high, low))

    for piece, mate_ref in enumerate(mate_refs):
        load_piece(piece + 1, mate_ref)
    own_copy.wait()
    load_piece(0, h_ref)
    weight_copy.wait()
    count_copy.wait()
    for group, members in enumerate(flips):
        for piece, (x_flip, c_flip) in enumerate(members):
            first_k = ((freq_pos ^ x_flip) * plan.group_devs + (group_pos ^ c_flip)) * k_local
            for local in range(k_local):
                weight = weight_ref[first_k + local].astype(jnp.float32)
                place = piece * k_local + local
                wr_ref[group, pl.ds(place, 1), :] = jnp.full((1, plan.width), weight, jnp.float32)

    def one_frequency(place, carry):
        offset = pl.multiple_of(place * orbitals, orbitals)

        def store(total):
            sum_ref[place] = total

        accumulate = sum_points(
            plan, masks, rows_ref[place], shift_ref[place],
            lambda item: t_ref[item, pl.ds(offset, orbitals), :],
            hd_ref[...], wr_ref[0], jnp.zeros((orbitals, plan.width), jnp.float32),
        )
        run_counts(count_ref[plan.freq_of(place)], accumulate, store)
        return carry

    lax.fori_loop(0, plan.lead, one_frequency, 0)


def near_kernel(plan, counts_ref, *refs):
    orbitals, width, sub, lead = plan.orbitals, plan.width, plan.sub, plan.lead
    steps = plan.z_devs - plan.lead_steps
    sg_refs, refs = refs[:steps], refs[steps:]
    old_refs, refs = refs[:5], refs[5:]
    hs_ref, hd_ref, wr_ref = refs[:3]
    new_refs, (t_ref, count_ref, sems) = refs[3:8], refs[8:]
    sum_ref, left_ref, right_ref, shift_ref, rows_ref = new_refs
    masks = Masks(orbitals)
    count_copy = fetch(counts_ref, count_ref, sems.at[0])
    for place in range(lead, plan.freqs):
        sg_ref = sg_refs[place // sub - plan.lead_steps]
        prepare_frequency(
            plan, masks, place, sg_ref[0, place % sub], sg_ref[1, place % sub], place,
            left_ref, right_ref, shift_ref, rows_ref,
        )
    lefts = left_ref[pl.ds(lead * orbitals, (plan.freqs - lead) * orbitals), :]
    for item in range(plan.k_total):
        tile = hs_ref[item]
        t_ref[item] = product(lefts, right_tile(tile[:, :width], tile[:, width:]))
    left_ref[pl.ds(0, lead * orbitals), :] = old_refs[1][...]
    for old_ref, new_ref in zip(old_refs, new_refs):
        if old_ref is not old_refs[1]:
            for place in range(lead):
                new_ref[place] = old_ref[place]
    count_copy.wait()

    def one_frequency(place, carry):
        offset = pl.multiple_of((place - lead) * orbitals, orbitals)

        def store(total):
            sum_ref[place] = total

        accumulate = sum_points(
            plan, masks, rows_ref[place], shift_ref[place],
            lambda item: t_ref[item, pl.ds(offset, orbitals), :],
            hd_ref[...], wr_ref[0], jnp.zeros((orbitals, width), jnp.float32),
        )
        run_counts(count_ref[plan.freq_of(place)], accumulate, store)
        return carry

    lax.fori_loop(lead, plan.freqs, one_frequency, 0)


def far_kernel(plan, group, pieces, counts_ref, weights_ref, *refs):
    k_local, orbitals, width, freqs = plan.k_local, plan.orbitals, plan.width, plan.freqs
    half = orbitals // 2
    h_refs, refs = refs[:pieces], refs[pieces:]
    old_ref, left_ref, right_ref, shift_ref, rows_ref, wr_ref = refs[:6]
    out_ref, t_ref, hd_ref, r_ref, plane_ref, weight_ref, count_ref, sems = refs[6:]
    masks = Masks(orbitals)
    count_copy = fetch(counts_ref, count_ref, sems.at[0])
    weight_copy = fetch(weights_ref, weight_ref, sems.at[1])
    for piece in range(pieces):
        for local in range(k_local):
            place = piece * k_local + local
            matrix = h_refs[piece][local]
            hd_ref[pl.ds(place, 1), :] = diagonal_row(masks, matrix)
            tile = right_tile(*split_bf16(block_form(matrix, masks.sign)))
            t_ref[place] = product(left_ref[...], tile)
    count_copy.wait()

    def one_frequency(place, carry):
        offset = pl.multiple_of(place * orbitals, orbitals)

        def store(total):
            r_ref[place] = total

        accumulate = sum_points(
            plan, masks, rows_ref[place], shift_ref[place],
            lambda item: t_ref[item, pl.ds(offset, orbitals), :],
            hd_ref[...], wr_ref[group], old_ref[place],
        )
        run_counts(count_ref[plan.freq_of(place)], accumulate, store)
        return carry

    if pieces:
        lax.fori_loop(0, freqs, one_frequency, 0)
    totals = r_ref if pieces else old_ref
    greens = []
    for place in range(freqs):
        tile = right_ref[place]
        right = right_tile(tile[:, :width], tile[:, width:])
        greens.append(product(left_tile(*split_bf16(totals[place])), right))
    weight_copy.wait()
    norm = 1.0 / jnp.sum(weight_ref[...].astype(jnp.float32), keepdims=True)
    for place, green in enumerate(greens):
        r_ref[place] = green * norm
    for place in range(freqs):
        even = r_ref[place, pl.ds(0, half, stride=2), :]
        odd = r_ref[place, pl.ds(1, half, stride=2), :]
        plane = plan.plane_of(place)
        real_rows = pl.multiple_of(plane * half, half)
        imag_rows = pl.multiple_of((freqs + plane) * half, half)
        plane_ref[pl.ds(real_rows, half), :] = jnp.where(masks.left_row, even, swap_halves(odd))
        plane_ref[pl.ds(imag_rows, half), :] = jnp.where(masks.left_row, swap_halves(even), odd)
    for line in range(half):
        out_ref[line] = plane_ref[pl.ds(line, 2 * freqs, stride=half), :]


def local_green(hamiltonian, self_energy, guess_factor, weights, counts):
    plan = Layout(hamiltonian, self_energy)
    orbitals, width, sub, freqs = plan.orbitals, plan.width, plan.sub, plan.freqs
    x_devs, z_devs, k_local = plan.x_devs, plan.z_devs, plan.k_local
    devices = plan.freq_devs * plan.group_devs
    pair_block = orbitals * orbitals // devices
    half = orbitals // 2
    c_pos = plan.positions()[2]

    def core_flip(values):
        return lax.ppermute(values, "kgrp", [(i, i ^ 1) for i in range(plan.group_devs)])

    def x_flip(values):
        return lax.ppermute(values, "freq", [(i, i ^ 1) for i in range(plan.freq_devs)])

    def z_move(values, step):
        pairs = []
        for i in range(plan.freq_devs):
            z_pos, x_pos = i // x_devs, i % x_devs
            target = z_pos ^ step if is_power_of_two(z_devs) else (z_pos + step) % z_devs
            pairs.append((i, target * x_devs + x_pos))
        return lax.ppermute(values, "freq", pairs)

    own = jnp.stack([self_energy, guess_factor])
    own = lax.dynamic_slice_in_dim(own, c_pos * sub, sub, 1)
    others = [z_move(own, step) for step in reversed(range(plan.lead_steps, z_devs))][::-1]
    leading = [own] + [z_move(own, step) for step in range(1, plan.lead_steps)]
    near, near_flips, far, far_flips = [hamiltonian], [(0, 0)], [], []
    if plan.c_devs == 2:
        near.append(core_flip(hamiltonian))
        near_flips.append((0, 1))
    if x_devs == 2:
        crossing, _ = lax.optimization_barrier((hamiltonian, own))
        far.append(x_flip(crossing))
        far_flips.append((1, 0))
        if plan.c_devs == 2:
            far_flips.append((1, 1))
    flips = (tuple(near_flips), tuple(far_flips))
    plan.k_total = len(near) * k_local
    k_rows = -(-plan.k_total // 8) * 8

    vmem = pl.BlockSpec(memory_space=pltpu.VMEM)
    outside = pl.BlockSpec(memory_space=pltpu.HBM)

    def in_hbm(values):
        return pltpu.with_memory_space_constraint(values, pltpu.HBM)

    count_scratch = pltpu.SMEM(counts.shape, counts.dtype)
    far_counts = in_hbm(counts)
    params = pltpu.CompilerParams(vmem_limit_bytes=40 * 1024 * 1024)

    estimate = pl.CostEstimate(flops=COST, bytes_accessed=1 << 20, transcendentals=0)

    def f32(*shape):
        return jax.ShapeDtypeStruct(shape, jnp.float32)

    def bf16(*shape):
        return jax.ShapeDtypeStruct(shape, jnp.bfloat16)

    def shared(places):
        return [
            f32(places, orbitals, width),
            bf16(places * orbitals, 2 * width),
            bf16(places, 2 * orbitals, 2 * width),
            f32(places, orbitals, width),
            f32(places, 8, width),
        ]

    outputs = shared(plan.lead) + [
        bf16(plan.k_total, 2 * orbitals, 2 * width), f32(k_rows, width), f32(2, k_rows, width)
    ]
    lead = pl.pallas_call(
        functools.partial(first_kernel, plan, flips),
        out_shape=outputs,
        in_specs=[outside] * 3 + [vmem] * (len(leading) + len(near) - 1),
        out_specs=[vmem] * len(outputs),
        scratch_shapes=[
            pltpu.VMEM((plan.k_total, plan.lead * orbitals, width), jnp.float32),
            pltpu.VMEM((k_local, orbitals, width), jnp.float32),
            pltpu.SMEM(weights.shape, weights.dtype),
            count_scratch,
            pltpu.SemaphoreType.DMA((3,)),
        ],
        compiler_params=params,
        cost_estimate=estimate,
        name="first",
    )
    *old, h_tiles, h_diags, w_rows = lead(
        in_hbm(weights), far_counts, in_hbm(hamiltonian), *leading, *near[1:]
    )
    outputs = shared(freqs)
    shares = pl.pallas_call(
        functools.partial(near_kernel, plan),
        out_shape=outputs,
        in_specs=[outside] + [vmem] * (len(others) + len(old) + 3),
        out_specs=[vmem] * len(outputs),
        scratch_shapes=[
            pltpu.VMEM((plan.k_total, (freqs - plan.lead) * orbitals, width), jnp.float32),
            count_scratch,
            pltpu.SemaphoreType.DMA((1,)),
        ],
        compiler_params=pltpu.CompilerParams(vmem_limit_bytes=40 * 1024 * 1024),
        cost_estimate=estimate,
        name="near",
    )(far_counts, *others, *old, h_tiles, h_diags, w_rows)
    if far and plan.c_devs == 2:
        crossed, _ = lax.optimization_barrier((far[0], w_rows))
        far.append(core_flip(crossed))
    partial_sums = pl.pallas_call(
        functools.partial(far_kernel, plan, 1, len(far)),
        out_shape=f32(half, 2 * freqs, width),
        in_specs=[outside] * 2 + [vmem] * (len(far) + len(shares) + 1),
        out_specs=vmem,
        scratch_shapes=[
            pltpu.VMEM((plan.k_total, freqs * orbitals, width), jnp.float32),
            pltpu.VMEM((k_rows, width), jnp.float32),
            pltpu.VMEM((freqs, orbitals, width), jnp.float32),
            pltpu.VMEM((2 * freqs * half, width), jnp.float32),
            pltpu.VMEM((1, weights.size), weights.dtype),
            count_scratch,
            pltpu.SemaphoreType.DMA((2,)),
        ],
        compiler_params=params,
        name="far",
    )(far_counts, in_hbm(weights.reshape(1, -1)), *far, *shares, w_rows)

    share = width // pair_block
    outgoing = partial_sums.reshape(half, 2 * freqs, share, pair_block).transpose(0, 2, 1, 3)
    outgoing = outgoing.reshape(devices, 2 * freqs, pair_block)
    arrived = lax.all_to_all(outgoing, ("freq", "kgrp"), 0, 0, tiled=True)
    parts = arrived.reshape(z_devs, x_devs, plan.y_devs, plan.c_devs, 2, z_devs, sub, pair_block)
    result = jnp.sum(parts, (0, 2)).transpose(2, 3, 0, 1, 4, 5)
    return result.reshape(2 * plan.freq_total, pair_block).T


def solution(mesh):
    return jax.shard_map(
        local_green,
        mesh=mesh,
        in_specs=(
            P(("freq", "kgrp"), None, None),
            P("freq", None, None),
            P("freq", None, None),
            P(),
            P(),
        ),
        out_specs=P(("freq", "kgrp"), None),
        check_vma=False,
    )
```

profile of v0, /device:TPU:0, one launch (start us, length us, event | category | flops | bytes accessed | tf_op | source)
XLA Modules:
  0.0 42.0 jit_solution(11857724649799536751)
XLA Ops:
  0.0 0.5 %collective-permute-start.2 = (f32[8,64,128]{2,1,0:T(8,128)}, f32[8,64,128]{2,1,0:T(8,128)S(1)}, u32[]{:S(2)}, u32[]{:S(2)}) collective-permute-start(f32[8,64,128]{2,1,0:T(8,128)} %own_ref.1), channel_id=1, source_target_pairs={{0,1},{1,0},{2,3},{3,2},{4,5},{5,4},{6,7},{7,6},{8,9},{9,8},{10,11... | collective-permute-start | bytes 786440 | tf_op jit(solution)/shard_map/ppermute | solution.py:379
  0.5 0.8 %fusion.refs_0_ = f32[2,1,64,128]{3,2,1,0:T(8,128)S(1)} fusion(s32[]{:T(128)S(6)} %select_n.11, f32[1,2,64,128]{3,2,1,0:T(8,128)} %bitcast.11, f32[1,2,64,128]{3,2,1,0:T(8,128)} %bitcast.12), kind=kLoop, calls=%fused_computation.2 | loop fusion | flops 16384 | bytes 196612 | tf_op jit(solution)/shard_map/stack | solution.py:392
  1.3 2.5 %collective-permute-start = (f32[8,64,128]{2,1,0:T(8,128)}, f32[8,64,128]{2,1,0:T(8,128)S(1)}, u32[]{:S(2)}, u32[]{:S(2)}) collective-permute-start(f32[8,64,128]{2,1,0:T(8,128)} %own_ref.1), channel_id=1, source_target_pairs={{0,4},{4,0},{8,12},{12,8},{16,20},{20,16},{24,28},{28,24},{1,5},{5... | collective-permute-start | bytes 786440 | tf_op jit(solution)/shard_map/ppermute | solution.py:382
  3.8 1.6 %collective-permute-start.1 = (f32[2,1,64,128]{3,2,1,0:T(8,128)S(1)}, f32[2,1,64,128]{3,2,1,0:T(8,128)S(1)}, u32[]{:S(2)}, u32[]{:S(2)}) collective-permute-start(f32[2,1,64,128]{3,2,1,0:T(8,128)S(1)} %fusion.refs_0_), channel_id=1, source_target_pairs={{0,8},{4,12},{8,0},{12,4},{16,24},{20,28},{24,16},{28,20},{1,9},{5... | collective-permute-start | bytes 196616 | tf_op jit(solution)/shard_map/ppermute | solution.py:390
  5.3 2.7 %collective-permute-done.1.refs_1_ = f32[2,1,64,128]{3,2,1,0:T(8,128)S(1)} collective-permute-done((f32[2,1,64,128]{3,2,1,0:T(8,128)S(1)}, f32[2,1,64,128]{3,2,1,0:T(8,128)S(1)}, u32[]{:S(2)}, u32[]{:S(2)}) %collective-permute-start.1) | collective-permute-done | bytes 65568 | tf_op jit(solution)/shard_map/ppermute | solution.py:390
  8.0 0.0 collective-permute-done.2.refs_2_
  8.0 3.6 %first.1 = (f32[2,64,128]{2,1,0:T(8,128)S(1)}, bf16[128,256]{1,0:T(8,128)(2,1)S(1)}, bf16[2,128,256]{2,1,0:T(8,128)(2,1)S(1)}, f32[2,64,128]{2,1,0:T(8,128)S(1)}...) custom-call(s32[256]{0:T(256)} %weights_ref.1, ...), custom_call_target="tpu_custom_call" | custom-call | flops 400000000 | bytes 1048576 | tf_op jit(solution)/shard_map/first/pallas_call | solution.py:456
  11.6 0.0 collective-permute-done.refs_0_
  11.6 0.1 collective-permute-start.3
  11.7 2.1 %collective-permute-start.4 = (f32[2,1,64,128]{3,2,1,0:T(8,128)S(1)}, f32[2,1,64,128]{3,2,1,0:T(8,128)S(1)}, u32[]{:S(2)}, u32[]{:S(2)}) collective-permute-start(f32[2,1,64,128]{3,2,1,0:T(8,128)S(1)} %fusion.refs_0_), channel_id=1, source_target_pairs={{0,16},{4,20},{8,24},{12,28},{16,0},{20,4},{24,8},{28,12},{1,17},{... | collective-permute-start | bytes 196616 | tf_op jit(solution)/shard_map/ppermute | solution.py:390
  13.8 1.9 %collective-permute-start.5 = (f32[2,1,64,128]{3,2,1,0:T(8,128)S(1)}, f32[2,1,64,128]{3,2,1,0:T(8,128)S(1)}, u32[]{:S(2)}, u32[]{:S(2)}) collective-permute-start(f32[2,1,64,128]{3,2,1,0:T(8,128)S(1)} %fusion.refs_0_), channel_id=1, source_target_pairs={{0,24},{4,28},{8,16},{12,20},{16,8},{20,12},{24,0},{28,4},{1,25},{... | collective-permute-start | bytes 196616 | tf_op jit(solution)/shard_map/ppermute | solution.py:390
  15.7 4.5 %collective-permute-done.4.refs_0_ = f32[2,1,64,128]{3,2,1,0:T(8,128)S(1)} collective-permute-done((f32[2,1,64,128]{3,2,1,0:T(8,128)S(1)}, f32[2,1,64,128]{3,2,1,0:T(8,128)S(1)}, u32[]{:S(2)}, u32[]{:S(2)}) %collective-permute-start.4) | collective-permute-done | bytes 65568 | tf_op jit(solution)/shard_map/ppermute | solution.py:390
  20.2 0.0 collective-permute-done.5.refs_1_
  20.2 2.3 %near.1 = (f32[4,64,128]{2,1,0:T(8,128)S(1)}, bf16[256,256]{1,0:T(8,128)(2,1)S(1)}, bf16[4,128,256]{2,1,0:T(8,128)(2,1)S(1)}, f32[4,64,128]{2,1,0:T(8,128)S(1)}, f32[4,8,128]{2,1,0:T(8,128)S(1)}) custom-call(s32[16]{0:T(128)} %counts_ref.5, f32[2,1,64,128]{3,2,1,0:T(8,128)S(1)} %collective-permute-done.4.refs_0_, ...), custom_call_target="tpu_custom_call" | custom-call | flops 400000000 | bytes 1048576 | tf_op jit(solution)/shard_map/near/pallas_call | solution.py:460
  22.5 0.0 collective-permute-done.3.refs_1_
  22.5 4.7 %far.1 = f32[32,8,128]{2,1,0:T(8,128)S(1)} custom-call(s32[16]{0:T(128)} %counts_ref.5, s32[1,256]{1,0:T(1,128)} %bitcast.14, f32[8,64,128]{2,1,0:T(8,128)S(1)} %collective-permute-done.refs_0_, f32[8,64,128]{2,1,0:T(8,128)S(1)} %collective-permute-done.3.refs_1_, f32[4,64,128]{2,1,0:T(8,128)S(1)} %get-tuple-element.30.refs_2_, ...), custom_call_target="tpu_custom_call" | custom-call | tf_op jit(solution)/shard_map/far/pallas_call | solution.py:477
  27.2 14.2 %all_to_all.5 = f32[32,8,128]{2,1,0:T(8,128)S(1)} all-to-all(f32[32,8,128]{2,1,0:T(8,128)S(1)} %far.1), channel_id=1, replica_groups=mesh['freq'=8,'kgrp'=4] {'freq','kgrp'}, dimensions={0} | all-to-all | bytes 262144 | tf_op jit(solution)/shard_map/all_to_all | solution.py:498
  41.4 0.6 %copy.6 = f32[2,4,2,2,1,128]{5,3,2,1,0,4:T(2,128)} copy(f32[2,4,2,2,1,128]{5,1,0,3,2,4:T(4,128)S(1)} %bitcast.13) | data formatting | bytes 32768 | tf_op jit(solution)/shard_map/transpose | solution.py:500
  (1 shorter events, 0.0 us)
Async XLA Ops:
  0.0 8.0 %collective-permute-start.2 = (f32[8,64,128]{2,1,0:T(8,128)}, f32[8,64,128]{2,1,0:T(8,128)S(1)}, u32[]{:S(2)}, u32[]{:S(2)}) collective-permute-start(f32[8,64,128]{2,1,0:T(8,128)} %own_ref.1), channel_id=1, source_target_pairs={{0,1},{1,0},{2,3},{3,2},{4,5},{5,4},{6,7},{7,6},{8,9},{9,8},{10,11... | collective-permute-start | bytes 786440 | tf_op jit(solution)/shard_map/ppermute | solution.py:379
  1.3 10.3 %collective-permute-start = (f32[8,64,128]{2,1,0:T(8,128)}, f32[8,64,128]{2,1,0:T(8,128)S(1)}, u32[]{:S(2)}, u32[]{:S(2)}) collective-permute-start(f32[8,64,128]{2,1,0:T(8,128)} %own_ref.1), channel_id=1, source_target_pairs={{0,4},{4,0},{8,12},{12,8},{16,20},{20,16},{24,28},{28,24},{1,5},{5... | collective-permute-start | bytes 786440 | tf_op jit(solution)/shard_map/ppermute | solution.py:382
  3.8 4.3 %collective-permute-start.1 = (f32[2,1,64,128]{3,2,1,0:T(8,128)S(1)}, f32[2,1,64,128]{3,2,1,0:T(8,128)S(1)}, u32[]{:S(2)}, u32[]{:S(2)}) collective-permute-start(f32[2,1,64,128]{3,2,1,0:T(8,128)S(1)} %fusion.refs_0_), channel_id=1, source_target_pairs={{0,8},{4,12},{8,0},{12,4},{16,24},{20,28},{24,16},{28,20},{1,9},{5... | collective-permute-start | bytes 196616 | tf_op jit(solution)/shard_map/ppermute | solution.py:390
  11.6 10.9 %collective-permute-start.3 = (f32[8,64,128]{2,1,0:T(8,128)S(1)}, f32[8,64,128]{2,1,0:T(8,128)S(1)}, u32[]{:S(2)}, u32[]{:S(2)}) collective-permute-start(f32[8,64,128]{2,1,0:T(8,128)S(1)} %collective-permute-done.refs_0_), channel_id=1, source_target_pairs={{0,1},{1,0},{2,3},{3,2},{4,5},{5,4},{6,7},{7,6},{8,9},{9,8},{10,11... | collective-permute-start | bytes 786440 | tf_op jit(solution)/shard_map/ppermute | solution.py:379
  11.7 8.5 %collective-permute-start.4 = (f32[2,1,64,128]{3,2,1,0:T(8,128)S(1)}, f32[2,1,64,128]{3,2,1,0:T(8,128)S(1)}, u32[]{:S(2)}, u32[]{:S(2)}) collective-permute-start(f32[2,1,64,128]{3,2,1,0:T(8,128)S(1)} %fusion.refs_0_), channel_id=1, source_target_pairs={{0,16},{4,20},{8,24},{12,28},{16,0},{20,4},{24,8},{28,12},{1,17},{... | collective-permute-start | bytes 196616 | tf_op jit(solution)/shard_map/ppermute | solution.py:390
  13.8 6.4 %collective-permute-start.5 = (f32[2,1,64,128]{3,2,1,0:T(8,128)S(1)}, f32[2,1,64,128]{3,2,1,0:T(8,128)S(1)}, u32[]{:S(2)}, u32[]{:S(2)}) collective-permute-start(f32[2,1,64,128]{3,2,1,0:T(8,128)S(1)} %fusion.refs_0_), channel_id=1, source_target_pairs={{0,24},{4,28},{8,16},{12,20},{16,8},{20,12},{24,0},{28,4},{1,25},{... | collective-permute-start | bytes 196616 | tf_op jit(solution)/shard_map/ppermute | solution.py:390
where the time goes:
time: 42.3 us; the launch traced here: 42 us
  blocking collectives  14.2 us (34%)
  Pallas kernels  10.6 us (25%)
  starting transfers between devices  8.62 us (20%)
  waiting for transfers between devices  7.18 us (17%)
  other arithmetic  0.81 us (2%)
  local copies, waits for them, and re-layouts  0.62 us (1%)
    all_to_all x1, blocking collectives, local_green(): arrived = lax.all_to_all(outgoing, ('freq', 'kgrp'), 0, 0, tiled=True)  14.2 us
    ppermute x3, waiting for transfers between devices, z_move(): return lax.ppermute(values, 'freq', pairs)  7.17 us
    ppermute x3, starting transfers between devices, z_move(): return lax.ppermute(values, 'freq', pairs)  5.58 us
    pallas_call x1, Pallas kernels, local_green(): pl.pallas_call(functools.partial(far_kernel, plan, 1, len(far)), out_shap...  4.71 us
    pallas_call x1, Pallas kernels, local_green(): lead(in_hbm(weights), far_counts, in_hbm(hamiltonian), *leading, *near[1:])  3.58 us
    ppermute x1, starting transfers between devices, x_flip(): lax.ppermute(values, 'freq', [(i, i ^ 1) for i in range(plan.freq_devs)])  2.48 us
    pallas_call x1, Pallas kernels, local_green(): pl.pallas_call(functools.partial(near_kernel, plan), out_shape=outputs, i...  2.3 us
  transfers between devices with their start and end apart: 6, of which 2 were waited for; matrix products, arithmetic and copies ran while one was open for 2% of the time, Pallas kernels for 14%

commit v1 on v0

--- a/solution.py
+++ b/solution.py
@@ -143,6 +143,8 @@
     d_real = real / modulus
     d_imag = -imag / modulus
     d_start = jnp.where(masks.left_row, d_real, d_imag) * weights
+    d_high = d_start.astype(jnp.bfloat16).astype(jnp.float32)
+    d_low = d_start - d_high
     d_turned = d_imag * masks.sign
     d_signed = d_real * masks.sign
 
@@ -156,21 +158,17 @@
             errors.append(split_bf16(masks.eye_block - jnp.concatenate([upper, lower], 0)))
         return errors
 
-    def advance(series, powers):
+    def advance(series, lefts, powers):
         next_series, next_powers = [], []
-        for start, (high, low) in zip(series, powers):
-            s_high, s_low = split_bf16(start)
-            stacked = jnp.concatenate([left_tile(s_high, s_low), left_tile(high[:orbitals], low[:orbitals])], 0)
+        for start, left, (high, low) in zip(series, lefts, powers):
+            stacked = jnp.concatenate([left, left_tile(high[:orbitals], low[:orbitals])], 0)
             both = product(stacked, right_tile(high, low))
             next_series.append(start + both[:orbitals])
             next_powers.append(split_block(both[orbitals:], masks.sign))
         return next_series, next_powers
 
-    def finish(total, series, powers):
-        lefts = [left_tile(*split_bf16(start)) for start in series]
+    def finish(total, lefts, powers):
         rights = [right_tile(*power) for power in powers]
-        for start in series:
-            total = total + start
         return total + product(jnp.concatenate(lefts, 1), jnp.concatenate(rights, 0))
 
     def accumulate(advances, total):
@@ -178,9 +176,23 @@
             items = range(begin, min(begin + BATCH, plan.k_total))
             series = [masks.eye_both * d_start[item:item + 1] for item in items]
             powers = errors_of(items)
+            lefts = [
+                left_tile(
+                    (masks.eye_both * d_high[item:item + 1]).astype(jnp.bfloat16),
+                    (masks.eye_both * d_low[item:item + 1]).astype(jnp.bfloat16),
+                )
+                for item in items
+            ]
             for _ in range(advances):
-                series, powers = advance(series, powers)
-            total = finish(total, series, powers)
+                series, powers = advance(series, lefts, powers)
+                lefts = [left_tile(*split_bf16(start)) for start in series]
+            if advances:
+                for start in series:
+                    total = total + start
+            else:
+                rows = d_start[begin:begin + len(items)]
+                total = total + masks.eye_both * jnp.sum(rows, 0, keepdims=True)
+            total = finish(total, lefts, powers)
         return total
 
     return lambda advances: accumulate(advances, total)

time: 42.3 us -> 42.2 us (level)
  no operation moved by 1% of the time
where the time goes in v1:
time: 42.2 us; the launch traced here: 42 us
  blocking collectives  14.2 us (34%)
  Pallas kernels  10.5 us (25%)
  starting transfers between devices  8.62 us (20%)
  waiting for transfers between devices  7.19 us (17%)
  other arithmetic  0.81 us (2%)
  local copies, waits for them, and re-layouts  0.62 us (1%)
    all_to_all x1, blocking collectives, local_green(): arrived = lax.all_to_all(outgoing, ('freq', 'kgrp'), 0, 0, tiled=True)  14.2 us
    ppermute x3, waiting for transfers between devices, z_move(): return lax.ppermute(values, 'freq', pairs)  7.18 us
    ppermute x3, starting transfers between devices, z_move(): return lax.ppermute(values, 'freq', pairs)  5.58 us
    pallas_call x1, Pallas kernels, local_green(): pl.pallas_call(functools.partial(far_kernel, plan, 1, len(far)), out_shap...  4.65 us
    pallas_call x1, Pallas kernels, local_green(): lead(in_hbm(weights), far_counts, in_hbm(hamiltonian), *leading, *near[1:])  3.56 us
    ppermute x1, starting transfers between devices, x_flip(): lax.ppermute(values, 'freq', [(i, i ^ 1) for i in range(plan.freq_devs)])  2.48 us
    pallas_call x1, Pallas kernels, local_green(): pl.pallas_call(functools.partial(near_kernel, plan), out_shape=outputs, i...  2.27 us
  transfers between devices with their start and end apart: 6, of which 2 were waited for; matrix products, arithmetic and copies ran while one was open for 2% of the time, Pallas kernels for 14%

profile of v1, /device:TPU:0, one launch (start us, length us, event | category | flops | bytes accessed | tf_op | source)
XLA Modules:
  0.0 42.0 jit_solution(3299148511312627484)
XLA Ops:
  0.0 0.5 %collective-permute-start.2 = (f32[8,64,128]{2,1,0:T(8,128)}, f32[8,64,128]{2,1,0:T(8,128)S(1)}, u32[]{:S(2)}, u32[]{:S(2)}) collective-permute-start(f32[8,64,128]{2,1,0:T(8,128)} %own_ref.1), channel_id=1, source_target_pairs={{0,1},{1,0},{2,3},{3,2},{4,5},{5,4},{6,7},{7,6},{8,9},{9,8},{10,11... | collective-permute-start | bytes 786440 | tf_op jit(solution)/shard_map/ppermute | solution.py:391
  0.5 0.8 %fusion.refs_0_ = f32[2,1,64,128]{3,2,1,0:T(8,128)S(1)} fusion(s32[]{:T(128)S(6)} %select_n.11, f32[1,2,64,128]{3,2,1,0:T(8,128)} %bitcast.11, f32[1,2,64,128]{3,2,1,0:T(8,128)} %bitcast.12), kind=kLoop, calls=%fused_computation.2 | loop fusion | flops 16384 | bytes 196612 | tf_op jit(solution)/shard_map/stack | solution.py:404
  1.3 2.5 %collective-permute-start = (f32[8,64,128]{2,1,0:T(8,128)}, f32[8,64,128]{2,1,0:T(8,128)S(1)}, u32[]{:S(2)}, u32[]{:S(2)}) collective-permute-start(f32[8,64,128]{2,1,0:T(8,128)} %own_ref.1), channel_id=1, source_target_pairs={{0,4},{4,0},{8,12},{12,8},{16,20},{20,16},{24,28},{28,24},{1,5},{5... | collective-permute-start | bytes 786440 | tf_op jit(solution)/shard_map/ppermute | solution.py:394
  3.8 1.6 %collective-permute-start.1 = (f32[2,1,64,128]{3,2,1,0:T(8,128)S(1)}, f32[2,1,64,128]{3,2,1,0:T(8,128)S(1)}, u32[]{:S(2)}, u32[]{:S(2)}) collective-permute-start(f32[2,1,64,128]{3,2,1,0:T(8,128)S(1)} %fusion.refs_0_), channel_id=1, source_target_pairs={{0,8},{4,12},{8,0},{12,4},{16,24},{20,28},{24,16},{28,20},{1,9},{5... | collective-permute-start | bytes 196616 | tf_op jit(solution)/shard_map/ppermute | solution.py:402
  5.3 2.7 %collective-permute-done.1.refs_1_ = f32[2,1,64,128]{3,2,1,0:T(8,128)S(1)} collective-permute-done((f32[2,1,64,128]{3,2,1,0:T(8,128)S(1)}, f32[2,1,64,128]{3,2,1,0:T(8,128)S(1)}, u32[]{:S(2)}, u32[]{:S(2)}) %collective-permute-start.1) | collective-permute-done | bytes 65568 | tf_op jit(solution)/shard_map/ppermute | solution.py:402
  8.0 0.0 collective-permute-done.2.refs_2_
  8.0 3.6 %first.1 = (f32[2,64,128]{2,1,0:T(8,128)S(1)}, bf16[128,256]{1,0:T(8,128)(2,1)S(1)}, bf16[2,128,256]{2,1,0:T(8,128)(2,1)S(1)}, f32[2,64,128]{2,1,0:T(8,128)S(1)}...) custom-call(s32[256]{0:T(256)} %weights_ref.1, ...), custom_call_target="tpu_custom_call" | custom-call | flops 400000000 | bytes 1048576 | tf_op jit(solution)/shard_map/first/pallas_call | solution.py:468
  11.6 0.0 collective-permute-done.refs_0_
  11.6 0.1 collective-permute-start.3
  11.7 2.1 %collective-permute-start.4 = (f32[2,1,64,128]{3,2,1,0:T(8,128)S(1)}, f32[2,1,64,128]{3,2,1,0:T(8,128)S(1)}, u32[]{:S(2)}, u32[]{:S(2)}) collective-permute-start(f32[2,1,64,128]{3,2,1,0:T(8,128)S(1)} %fusion.refs_0_), channel_id=1, source_target_pairs={{0,16},{4,20},{8,24},{12,28},{16,0},{20,4},{24,8},{28,12},{1,17},{... | collective-permute-start | bytes 196616 | tf_op jit(solution)/shard_map/ppermute | solution.py:402
  13.8 1.9 %collective-permute-start.5 = (f32[2,1,64,128]{3,2,1,0:T(8,128)S(1)}, f32[2,1,64,128]{3,2,1,0:T(8,128)S(1)}, u32[]{:S(2)}, u32[]{:S(2)}) collective-permute-start(f32[2,1,64,128]{3,2,1,0:T(8,128)S(1)} %fusion.refs_0_), channel_id=1, source_target_pairs={{0,24},{4,28},{8,16},{12,20},{16,8},{20,12},{24,0},{28,4},{1,25},{... | collective-permute-start | bytes 196616 | tf_op jit(solution)/shard_map/ppermute | solution.py:402
  15.7 4.5 %collective-permute-done.4.refs_0_ = f32[2,1,64,128]{3,2,1,0:T(8,128)S(1)} collective-permute-done((f32[2,1,64,128]{3,2,1,0:T(8,128)S(1)}, f32[2,1,64,128]{3,2,1,0:T(8,128)S(1)}, u32[]{:S(2)}, u32[]{:S(2)}) %collective-permute-start.4) | collective-permute-done | bytes 65568 | tf_op jit(solution)/shard_map/ppermute | solution.py:402
  20.2 0.0 collective-permute-done.5.refs_1_
  20.2 2.3 %near.1 = (f32[4,64,128]{2,1,0:T(8,128)S(1)}, bf16[256,256]{1,0:T(8,128)(2,1)S(1)}, bf16[4,128,256]{2,1,0:T(8,128)(2,1)S(1)}, f32[4,64,128]{2,1,0:T(8,128)S(1)}, f32[4,8,128]{2,1,0:T(8,128)S(1)}) custom-call(s32[16]{0:T(128)} %counts_ref.5, f32[2,1,64,128]{3,2,1,0:T(8,128)S(1)} %collective-permute-done.4.refs_0_, ...), custom_call_target="tpu_custom_call" | custom-call | flops 400000000 | bytes 1048576 | tf_op jit(solution)/shard_map/near/pallas_call | solution.py:472
  22.5 0.0 collective-permute-done.3.refs_1_
  22.5 4.6 %far.1 = f32[32,8,128]{2,1,0:T(8,128)S(1)} custom-call(s32[16]{0:T(128)} %counts_ref.5, s32[1,256]{1,0:T(1,128)} %bitcast.14, f32[8,64,128]{2,1,0:T(8,128)S(1)} %collective-permute-done.refs_0_, f32[8,64,128]{2,1,0:T(8,128)S(1)} %collective-permute-done.3.refs_1_, f32[4,64,128]{2,1,0:T(8,128)S(1)} %get-tuple-element.30.refs_2_, ...), custom_call_target="tpu_custom_call" | custom-call | tf_op jit(solution)/shard_map/far/pallas_call | solution.py:489
  27.1 14.2 %all_to_all.5 = f32[32,8,128]{2,1,0:T(8,128)S(1)} all-to-all(f32[32,8,128]{2,1,0:T(8,128)S(1)} %far.1), channel_id=1, replica_groups=mesh['freq'=8,'kgrp'=4] {'freq','kgrp'}, dimensions={0} | all-to-all | bytes 262144 | tf_op jit(solution)/shard_map/all_to_all | solution.py:510
  41.4 0.6 %copy.6 = f32[2,4,2,2,1,128]{5,3,2,1,0,4:T(2,128)} copy(f32[2,4,2,2,1,128]{5,1,0,3,2,4:T(4,128)S(1)} %bitcast.13) | data formatting | bytes 32768 | tf_op jit(solution)/shard_map/transpose | solution.py:512
  (1 shorter events, 0.0 us)
Async XLA Ops:
  0.0 8.0 %collective-permute-start.2 = (f32[8,64,128]{2,1,0:T(8,128)}, f32[8,64,128]{2,1,0:T(8,128)S(1)}, u32[]{:S(2)}, u32[]{:S(2)}) collective-permute-start(f32[8,64,128]{2,1,0:T(8,128)} %own_ref.1), channel_id=1, source_target_pairs={{0,1},{1,0},{2,3},{3,2},{4,5},{5,4},{6,7},{7,6},{8,9},{9,8},{10,11... | collective-permute-start | bytes 786440 | tf_op jit(solution)/shard_map/ppermute | solution.py:391
  1.3 10.3 %collective-permute-start = (f32[8,64,128]{2,1,0:T(8,128)}, f32[8,64,128]{2,1,0:T(8,128)S(1)}, u32[]{:S(2)}, u32[]{:S(2)}) collective-permute-start(f32[8,64,128]{2,1,0:T(8,128)} %own_ref.1), channel_id=1, source_target_pairs={{0,4},{4,0},{8,12},{12,8},{16,20},{20,16},{24,28},{28,24},{1,5},{5... | collective-permute-start | bytes 786440 | tf_op jit(solution)/shard_map/ppermute | solution.py:394
  3.8 4.3 %collective-permute-start.1 = (f32[2,1,64,128]{3,2,1,0:T(8,128)S(1)}, f32[2,1,64,128]{3,2,1,0:T(8,128)S(1)}, u32[]{:S(2)}, u32[]{:S(2)}) collective-permute-start(f32[2,1,64,128]{3,2,1,0:T(8,128)S(1)} %fusion.refs_0_), channel_id=1, source_target_pairs={{0,8},{4,12},{8,0},{12,4},{16,24},{20,28},{24,16},{28,20},{1,9},{5... | collective-permute-start | bytes 196616 | tf_op jit(solution)/shard_map/ppermute | solution.py:402
  11.6 10.9 %collective-permute-start.3 = (f32[8,64,128]{2,1,0:T(8,128)S(1)}, f32[8,64,128]{2,1,0:T(8,128)S(1)}, u32[]{:S(2)}, u32[]{:S(2)}) collective-permute-start(f32[8,64,128]{2,1,0:T(8,128)S(1)} %collective-permute-done.refs_0_), channel_id=1, source_target_pairs={{0,1},{1,0},{2,3},{3,2},{4,5},{5,4},{6,7},{7,6},{8,9},{9,8},{10,11... | collective-permute-start | bytes 786440 | tf_op jit(solution)/shard_map/ppermute | solution.py:391
  11.7 8.5 %collective-permute-start.4 = (f32[2,1,64,128]{3,2,1,0:T(8,128)S(1)}, f32[2,1,64,128]{3,2,1,0:T(8,128)S(1)}, u32[]{:S(2)}, u32[]{:S(2)}) collective-permute-start(f32[2,1,64,128]{3,2,1,0:T(8,128)S(1)} %fusion.refs_0_), channel_id=1, source_target_pairs={{0,16},{4,20},{8,24},{12,28},{16,0},{20,4},{24,8},{28,12},{1,17},{... | collective-permute-start | bytes 196616 | tf_op jit(solution)/shard_map/ppermute | solution.py:402
  13.8 6.4 %collective-permute-start.5 = (f32[2,1,64,128]{3,2,1,0:T(8,128)S(1)}, f32[2,1,64,128]{3,2,1,0:T(8,128)S(1)}, u32[]{:S(2)}, u32[]{:S(2)}) collective-permute-start(f32[2,1,64,128]{3,2,1,0:T(8,128)S(1)} %fusion.refs_0_), channel_id=1, source_target_pairs={{0,24},{4,28},{8,16},{12,20},{16,8},{20,12},{24,0},{28,4},{1,25},{... | collective-permute-start | bytes 196616 | tf_op jit(solution)/shard_map/ppermute | solution.py:402
